TPU v7x, 8 devices: a whole 2x2x1 slice. The times are simulated.
8 devices in a mesh: dp: 1 (over z), tp: 8 (over x, y, core).
Axes of the slice: x: 2, y: 2, z: 1, core: 2. Of those that a mesh axis runs over, the one named last changes fastest.
Arguments:
- x: bfloat16 [2048, 2048], P('dp')
- dy: bfloat16 [2048, 2048], P('dp')
- gate: bfloat16 [2048, 6144], P('dp', 'tp')
- up: bfloat16 [2048, 6144], P('dp', 'tp')
- w_gate: bfloat16 [2048, 6144], P(None, 'tp')
- w_up: bfloat16 [2048, 6144], P(None, 'tp')
- w_down: bfloat16 [6144, 2048], P('tp')
Outputs:
- output 1: bfloat16 [2048, 2048], P('dp')
- output 2: bfloat16 [2048, 6144], P('dp', 'tp')
- output 3: bfloat16 [2048, 6144], P('dp', 'tp')
- output 4: bfloat16 [6144, 2048], P(('dp', 'tp'))
All inputs are finite; a program needn't handle non-finite values.
Results may differ from a plain program's by a relative error of at most 0.012.
Values are sent between devices in bfloat16 or wider.
A program may use at most 2 GiB of HBM per device.

v0:
```python
import jax
import jax.numpy as jnp
from jax import lax
from jax.sharding import PartitionSpec as P


def act(gate, up):
    return jax.nn.silu(gate) * up


def solution(mesh):
    def step(x, dy, gate, up, w_gate, w_up, w_down):
        hidden, back = jax.vjp(act, gate.astype(jnp.float32), up.astype(jnp.float32))
        d_hidden = jnp.dot(dy, w_down.T, preferred_element_type=jnp.float32)
        d_gate, d_up = (g.astype(jnp.bfloat16) for g in back(d_hidden))
        term = jnp.dot(d_gate, w_gate.T, preferred_element_type=jnp.float32) + jnp.dot(d_up, w_up.T, preferred_element_type=jnp.float32)
        dx = lax.psum(term.astype(jnp.bfloat16), "tp")
        dw_gate = jnp.dot(x.T, d_gate, preferred_element_type=jnp.float32)
        dw_up = jnp.dot(x.T, d_up, preferred_element_type=jnp.float32)
        dw_down = jnp.dot(hidden.astype(jnp.bfloat16).T, dy, preferred_element_type=jnp.float32)
        return dx, *(g.astype(jnp.bfloat16) for g in (dw_gate, dw_up, dw_down))

    tokens, columns, rows = P("dp", None), P(None, "tp"), P("tp", None)
    return jax.shard_map(
        step,
        mesh=mesh,
        in_specs=(tokens, tokens, P("dp", "tp"), P("dp", "tp"), columns, columns, rows),
        out_specs=(tokens, P("dp", "tp"), P("dp", "tp"), P(("dp", "tp"), None)),
        check_vma=False,
    )
```

profile of v0, /device:TPU:0, one launch (start us, length us, event | category | flops | bytes accessed | tf_op | source)
XLA Modules:
  0.0 180.9 jit_solution(2669897494385128676)
XLA Ops:
  7.2 0.0 copy-start
  7.2 0.0 all-reduce.2.cloned.1.call-start
  7.2 14.7 %fusion.6 = (bf16[2048,768]{1,0:T(8,128)(2,1)S(1)}, f32[2048,768]{1,0:T(8,128)}) fusion(bf16[2048,768]{1,0:T(8,128)(2,1)} %param.9, bf16[2048,768]{1,0:T(8,128)(2,1)} %param.10, bf16[2048,2048]{1,0:T(8,128)(2,1)} %param.8, bf16[768,2048]{1,0:T(8,128)(2,1)} %param.13), kind=kOutput, calls=%fused_computation.13 | convolution fusion | flops 6462898176 | bytes 27262976 | tf_op jit(solution)/shard_map/dot_general | solution.py:14
  21.9 0.0 copy-start.2
  21.9 0.0 copy-done
  21.9 9.6 %fusion.11 = f32[2048,2048]{1,0:T(8,128)} fusion(bf16[2048,768]{1,0:T(8,128)(2,1)S(1)} %get-tuple-element.8, bf16[2048,768]{1,0:T(8,128)(2,1)S(1)} %copy-done), kind=kOutput, calls=%fused_computation.21 | convolution fusion | flops 6442450944 | bytes 23068672 | tf_op jit(solution)/shard_map/dot_general | solution.py:16
  31.5 0.0 copy-done.2
  31.5 16.4 %add_convert_fusion = bf16[2048,2048]{1,0:T(8,128)(2,1)} fusion(f32[2048,2048]{1,0:T(8,128)} %fusion.11, bf16[2048,768]{1,0:T(8,128)(2,1)} %param.12, f32[2048,768]{1,0:T(8,128)} %get-tuple-element.9, bf16[2048,768]{1,0:T(8,128)(2,1)} %param.9), kind=kOutput, calls=%fused_computation | convolution fusion | flops 6461849600 | bytes 37748736 | tf_op jit(solution)/shard_map/dot_general | solution.py:16
  47.9 0.0 all-reduce.2.cloned.1.call-update
  48.0 10.1 %fusion.8 = bf16[2048,768]{0,1:T(8,128)(2,1)S(1)} fusion(bf16[2048,768]{1,0:T(8,128)(2,1)} %copy-done.2, bf16[2048,2048]{1,0:T(8,128)(2,1)} %param.7), kind=kOutput, calls=%fused_computation.18 | convolution fusion | flops 6444023808 | bytes 14680064 | tf_op jit(solution)/shard_map/dot_general | solution.py:18
  58.1 2.8 %copy.11 = bf16[2048,768]{1,0:T(8,128)(2,1)} copy(bf16[2048,768]{0,1:T(8,128)(2,1)S(1)} %fusion.8) | data formatting | bytes 6291456
  60.9 12.4 %fusion.9 = bf16[2048,768]{0,1:T(8,128)(2,1)S(1)} fusion(bf16[2048,2048]{1,0:T(8,128)(2,1)} %param.7, f32[2048,768]{1,0:T(8,128)} %get-tuple-element.9, bf16[2048,768]{1,0:T(8,128)(2,1)} %param.9), kind=kOutput, calls=%fused_computation.19 | convolution fusion | flops 6455033856 | bytes 20971520 | tf_op jit(solution)/shard_map/dot_general | solution.py:19
  73.4 2.8 %copy.12 = bf16[2048,768]{1,0:T(8,128)(2,1)} copy(bf16[2048,768]{0,1:T(8,128)(2,1)S(1)} %fusion.9) | data formatting | bytes 6291456
  76.2 0.0 copy-start.1
  76.2 13.3 %convolution_convert_fusion = bf16[768,2048]{1,0:T(8,128)(2,1)} fusion(bf16[2048,2048]{1,0:T(8,128)(2,1)} %param.8, bf16[2048,768]{1,0:T(8,128)(2,1)} %param.10, bf16[2048,768]{1,0:T(8,128)(2,1)} %param.9), kind=kOutput, calls=%fused_computation.15 | convolution fusion | flops 6456606720 | bytes 17825792 | tf_op jit(solution)/shard_map/dot_general | solution.py:20
  89.5 76.1 %all-reduce.2.cloned.1.call-done = bf16[2048,2048]{1,0:T(8,128)(2,1)} async-done(((bf16[2048,2048]{1,0:T(8,128)(2,1)}), bf16[2048,2048]{1,0:T(8,128)(2,1)}) %all-reduce.2.cloned.1.call-update) | async-done | bytes 8388624 | tf_op jit(solution)/shard_map/psum | solution.py:17
  165.6 8.4 %copy.14 = bf16[2048,2048]{1,0:T(8,128)(2,1)} copy(bf16[2048,2048]{1,0:T(8,128)(2,1)} %all-reduce.2.cloned.1.call-done) | data formatting | bytes 16777216
  174.0 0.0 copy-done.1
Async XLA Ops:
  7.2 14.7 %copy-start = (bf16[2048,768]{1,0:T(8,128)(2,1)S(1)}, bf16[2048,768]{1,0:T(8,128)(2,1)}, u32[]{:S(2)}) copy-start(bf16[2048,768]{1,0:T(8,128)(2,1)} %param.11) | copy-start | bytes 9437188
  7.2 158.4 %all-reduce.2.cloned.1.call-start = ((), (), s32[]{:S(2)}) async-start(), calls=%async_computation | async-start | bytes 16777216 | tf_op jit(solution)/shard_map/psum | solution.py:17
  21.9 9.6 %copy-start.2 = (bf16[2048,768]{1,0:T(8,128)(2,1)}, bf16[2048,768]{1,0:T(8,128)(2,1)S(1)}, u32[]{:S(2)}) copy-start(bf16[2048,768]{1,0:T(8,128)(2,1)S(1)} %get-tuple-element.8) | copy-start | bytes 9437188
  76.2 97.9 %copy-start.1 = (bf16[2048,768]{1,0:T(8,128)(2,1)S(1)}, bf16[2048,768]{1,0:T(8,128)(2,1)}, u32[]{:S(2)}) copy-start(bf16[2048,768]{1,0:T(8,128)(2,1)} %param.11) | copy-start | bytes 9437188
Sparse Core Ops, SparseCore 0:
  48.1 117.4 all-reduce.1
where the time goes:
time: 181 us
  matrix products  76.6 us (42%)
  waiting for transfers between devices  76.2 us (42%)
  between operations  14.1 us (8%)
  local copies, waits for them, and re-layouts  14 us (8%)
    psum x1, waiting for transfers between devices, step(): dx = lax.psum(term.astype(jnp.bfloat16), 'tp')  76.1 us
    dot_general x1, matrix products, step(): jnp.dot(d_up, w_up.T, preferred_element_type=jnp.float32)  16.4 us
    dot_general x1, matrix products, step(): d_hidden = jnp.dot(dy, w_down.T, preferred_element_type=jnp.float32)  14.7 us
    unnamed x9, local copies, waits for them, and re-layouts  14 us
    dot_general x1, matrix products, step(): jnp.dot(hidden.astype(jnp.bfloat16).T, dy, preferred_element_type=jnp.flo...  13.3 us
    dot_general x1, matrix products, step(): dw_up = jnp.dot(x.T, d_up, preferred_element_type=jnp.float32)  12.4 us
    dot_general x1, matrix products, step(): dw_gate = jnp.dot(x.T, d_gate, preferred_element_type=jnp.float32)  10.1 us
    dot_general x1, matrix products, step(): jnp.dot(d_gate, w_gate.T, preferred_element_type=jnp.float32)  9.59 us
  transfers between devices with their start and end apart: 1, of which 1 were waited for; matrix products, arithmetic and copies ran while one was open for 23% of the time, Pallas kernels for 0%

commit v1 on v0

v1 whole, which is shorter than its diff:
```python
import jax
import jax.numpy as jnp
from jax import lax
from jax.experimental import pallas as pl
from jax.experimental.pallas import tpu as pltpu
from jax.sharding import PartitionSpec as P

MESH = pl.DeviceIdType.MESH
BF, F32 = jnp.bfloat16, jnp.float32
NT = (((1,), (1,)), ((), ()))
TN = (((0,), (0,)), ((), ()))

ROWS, D, HID = 2048, 2048, 768
R = 256
C = ROWS // R
R2, R4 = R // 2, R // 4
OWN = D // 2
HC = OWN // 2
XB = 256
ACC, SS, XS = 4, 2, 3
LAG = 5

D2D, RS1, RS2, AG1, AG2, FIN = 0, 2, 4, 6, 8, 10
KINDS = 11


def dot(a, b, dims):
    return lax.dot_general(a, b, dims, preferred_element_type=F32)


def al(v, m):
    return pl.multiple_of(v, m)


def kernel(x, dy, gate, up, w_gate, w_up, w_down, dx, dwg, dwu, dwd,
           dyv, gv, uv, dg, du, hid, xv, acc, d2d_s, d2d_r, rs1_s, rs1_r, rs2_s, rs2_r,
           send, recv, lw, lc, lx):
    me = lax.axis_index("tp")
    c, y, xx = me % 2, (me // 2) % 2, me // 4
    partner = {"tp": me + 1 - 2 * c}
    ny = {"tp": me + 2 - 4 * y}
    nx = {"tp": me + 4 - 8 * xx}
    first, second = (xx, y), (y, xx)
    to_first, to_second = (nx, ny), (ny, nx)

    def load_chunk(k):
        slot = k % 2
        r = pl.ds(al(k * R, R), R)
        return [pltpu.make_async_copy(dy.at[r], dyv.at[r], lc.at[slot, 0]),
                pltpu.make_async_copy(gate.at[r], gv.at[slot], lc.at[slot, 1]),
                pltpu.make_async_copy(up.at[r], uv.at[slot], lc.at[slot, 2])]

    def load_x(j):
        slot = j % XS
        return pltpu.make_async_copy(x.at[:, pl.ds(al(j * XB, XB), XB)], xv.at[slot], lx.at[slot])

    def load_down(i):
        r = pl.ds(i * 256, 256)
        return pltpu.make_async_copy(w_down.at[r], dwd.at[r], lw.at[i])

    def wrows(own, h):
        return pl.ds(al((c if own else 1 - c) * OWN + h * HC, HC), HC)

    def load_w(own, h):
        r = wrows(own, h)
        i = 3 + 2 * (2 * own + h)
        return [pltpu.make_async_copy(w_gate.at[r], dwg.at[r], lw.at[i]),
                pltpu.make_async_copy(w_up.at[r], dwu.at[r], lw.at[i + 1])]

    def rc(src, dst, k, kind, dev):
        return pltpu.make_async_remote_copy(src, dst, send.at[k, kind], recv.at[k, kind],
                                            device_id=dev, device_id_type=MESH)

    def cols(h):
        return pl.ds(al(c * OWN + h * HC, HC), HC)

    def cp(k, kind, h=0):
        if kind == D2D:
            return rc(d2d_s.at[k % SS, h], d2d_r.at[k, h], k, kind + h, partner)
        if kind == RS1:
            return rc(rs1_s.at[k, h], rs1_r.at[k, h], k, kind + h, to_first[h])
        if kind == RS2:
            return rc(rs2_s.at[k, h], rs2_r.at[k, h], k, kind + h, to_second[h])
        if kind == AG1:
            b = dx.at[pl.ds(al(k * R + first[h] * R2 + second[h] * R4, R4), R4), cols(h)]
            return rc(b, b, k, kind + h, to_second[h])
        if kind == AG2:
            b = dx.at[pl.ds(al(k * R + first[h] * R2, R2), R2), cols(h)]
            return rc(b, b, k, kind + h, to_first[h])
        b = dx.at[pl.ds(al(k * R, R), R), pl.ds(al(c * OWN, OWN), OWN)]
        return rc(b, b, k, kind, partner)

    def hidden(k, i):
        r, n = pl.ds(al(k * R, R), R), slice(i * 256, (i + 1) * 256)
        slot = k % 2
        dh = dot(dyv[r, :], dwd[n, :], NT)
        g, u = gv[slot, :, n].astype(F32), uv[slot, :, n].astype(F32)
        s = jax.nn.sigmoid(g)
        silu = g * s
        hid[r, n] = (silu * u).astype(BF)
        du[r, n] = (dh * silu).astype(BF)
        dg[r, n] = (dh * u * (s + silu * (1.0 - s))).astype(BF)

    def term(k, own, h):
        r = pl.ds(al(k * R, R), R)
        w = wrows(own, h)
        t = dot(dg[r, :], dwg[w, :], NT) + dot(du[r, :], dwu[w, :], NT)
        if own:
            acc[k % ACC, h] = t
        else:
            d2d_s[k % SS, h] = t.astype(BF)

    def sum1(k):
        for h in range(2):
            cp(k, D2D, h).wait_recv()
        for h in range(2):
            keep, leave = (pl.ds(al(v * R2, R2), R2) for v in (first[h], 1 - first[h]))
            acc[k % ACC, h, keep] = acc[k % ACC, h, keep] + d2d_r[k, h, keep].astype(F32)
            rs1_s[k, h] = (acc[k % ACC, h, leave] + d2d_r[k, h, leave].astype(F32)).astype(BF)

    def sum2(k):
        for h in range(2):
            cp(k, RS1, h).wait_recv()
        for h in range(2):
            a, b = second[h], 1 - second[h]
            keep, leave = (pl.ds(al(first[h] * R2 + v * R4, R4), R4) for v in (a, b))
            rkeep, rleave = (pl.ds(al(v * R4, R4), R4) for v in (a, b))
            acc[k % ACC, h, keep] = acc[k % ACC, h, keep] + rs1_r[k, h, rkeep].astype(F32)
            rs2_s[k, h] = (acc[k % ACC, h, leave] + rs1_r[k, h, rleave].astype(F32)).astype(BF)

    def sum3(k):
        for h in range(2):
            cp(k, RS2, h).wait_recv()
        for h in range(2):
            p = first[h] * R2 + second[h] * R4
            dx[pl.ds(al(k * R + p, R4), R4), cols(h)] = (
                acc[k % ACC, h, pl.ds(al(p, R4), R4)] + rs2_r[k, h].astype(F32)).astype(BF)

    def go(k, kind):
        for h in range(2):
            cp(k, kind, h).start()

    def gather2(k):
        for h in range(2):
            cp(k, AG1, h).wait_recv()
        go(k, AG2)

    def gather3(k):
        for h in range(2):
            cp(k, AG2, h).wait_recv()
        cp(k, FIN).start()

    barrier = pltpu.get_barrier_semaphore()
    for dev in (partner, ny, nx):
        pl.semaphore_signal(barrier, inc=1, device_id=dev, device_id_type=MESH)

    zero = jnp.int32(0)
    load_down(0).start()
    for l in load_chunk(zero):
        l.start()
    load_down(1).start()
    load_down(2).start()

    def step(k, static):
        if static == 0:
            load_down(0).wait()
            for l in load_chunk(k):
                l.wait()
            for h in range(2):
                for l in load_w(0, h):
                    l.start()
            hidden(k, 0)
            load_down(1).wait()
            for h in range(2):
                for l in load_w(1, h):
                    l.start()
            hidden(k, 1)
            load_down(2).wait()
            for l in load_chunk(k + 1):
                l.start()
            hidden(k, 2)
        else:
            for l in load_chunk(k):
                l.wait()
            sum1(k - 1)
            hidden(k, 0)
            go(k - 1, RS1)
            if static is not None:
                for l in load_chunk(k + 1):
                    l.start()
            else:
                @pl.when(k + 1 < C)
                def _():
                    for l in load_chunk(k + 1):
                        l.start()
            hidden(k, 1)
            hidden(k, 2)
        for h in range(2):
            if static == 0:
                for l in load_w(0, h):
                    l.wait()
                if h == 0:
                    pl.semaphore_wait(barrier, 3)
            if static is None or static >= SS:
                cp(k - SS, D2D, h).wait_send()
            term(k, 0, h)
            cp(k, D2D, h).start()
        if static == 0:
            for h in range(2):
                for l in load_w(1, h):
                    l.wait()
        if static is None or static >= 2:
            sum2(k - 2)
        term(k, 1, 0)
        if static is None or static >= 2:
            go(k - 2, RS2)
        if static is None or static >= 3:
            sum3(k - 3)
        term(k, 1, 1)
        if static is None:
            @pl.when(k >= LAG)
            def _():
                go(k - LAG, AG1)

    for k in range(3):
        step(jnp.int32(k), k)
        if k == 1:
            for j in range(XS):
                load_x(jnp.int32(j)).start()

    @pl.loop(3, C)
    def _(k):
        step(k, None)

    def wg(j, out, d):
        out[pl.ds(al(j * XB, XB), XB), :] = dot(xv[j % XS], d[...], TN).astype(BF)

    def wd(j):
        n = pl.ds(al(j * XB, XB), XB)
        dwd[:, n] = dot(hid[...], dyv[:, n], TN).astype(BF)

    i32 = jnp.int32
    j = i32(0)
    load_x(j).wait()
    sum1(i32(C - 1))
    wg(j, dwg, dg)
    go(i32(C - 1), RS1)
    gather2(i32(0))
    sum2(i32(C - 2))
    wg(j, dwu, du)
    go(i32(C - 2), RS2)
    load_x(j + XS).start()
    go(i32(C - LAG), AG1)
    sum3(i32(C - 3))
    wd(j)
    go(i32(C - LAG + 1), AG1)
    gather2(i32(1))
    j = i32(1)
    load_x(j).wait()
    sum2(i32(C - 1))
    wg(j, dwg, dg)
    go(i32(C - 1), RS2)
    sum3(i32(C - 2))
    wg(j, dwu, du)
    load_x(j + XS).start()
    go(i32(C - LAG + 2), AG1)
    gather2(i32(2))
    wd(j)
    j = i32(2)
    load_x(j).wait()
    sum3(i32(C - 1))
    wg(j, dwg, dg)
    go(i32(C - LAG + 3), AG1)
    go(i32(C - LAG + 4), AG1)
    gather2(i32(3))
    wg(j, dwu, du)
    load_x(j + XS).start()
    gather3(i32(0))
    wd(j)

    @pl.loop(3, C)
    def _(j):
        load_x(j).wait()
        wg(j, dwg, dg)

        @pl.when(j + 1 < C)
        def _():
            gather2(j + 1)

        wg(j, dwu, du)

        @pl.when(j + XS < C)
        def _():
            load_x(j + XS).start()

        gather3(j - 2)
        wd(j)

    gather3(i32(C - 2))
    gather3(i32(C - 1))

    @pl.loop(0, C)
    def _(k):
        @pl.when(k >= C - SS)
        def _():
            for h in range(2):
                cp(k, D2D, h).wait_send()

        for kind in (RS1, RS2, AG1, AG2):
            for h in range(2):
                cp(k, kind, h).wait_send()
        cp(k, FIN).wait()


def put(*refs):
    n = len(refs) // 2
    sem = refs[-1]
    copies = [pltpu.make_async_copy(refs[i], refs[n + i], sem.at[i]) for i in range(n)]
    for cpy in copies:
        cpy.start()
    for cpy in copies:
        cpy.wait()


def solution(mesh):
    shapes = [(ROWS, D), (D, HID), (D, HID), (HID, D)]

    def step(*args):
        outs = pl.pallas_call(
            kernel,
            out_shape=[pltpu.VMEM(s, BF) for s in shapes],
            in_specs=[pl.BlockSpec(memory_space=pltpu.HBM)] * 7,
            out_specs=[pl.BlockSpec(memory_space=pltpu.VMEM)] * 4,
            scratch_shapes=[
                pltpu.VMEM((ROWS, D), BF),
                pltpu.VMEM((2, R, HID), BF),
                pltpu.VMEM((2, R, HID), BF),
                pltpu.VMEM((ROWS, HID), BF),
                pltpu.VMEM((ROWS, HID), BF),
                pltpu.VMEM((ROWS, HID), BF),
                pltpu.VMEM((XS, ROWS, XB), BF),
                pltpu.VMEM((ACC, 2, R, HC), F32),
                pltpu.VMEM((SS, 2, R, HC), BF),
                pltpu.VMEM((C, 2, R, HC), BF),
                pltpu.VMEM((C, 2, R2, HC), BF),
                pltpu.VMEM((C, 2, R2, HC), BF),
                pltpu.VMEM((C, 2, R4, HC), BF),
                pltpu.VMEM((C, 2, R4, HC), BF),
                pltpu.SemaphoreType.DMA((C, KINDS)),
                pltpu.SemaphoreType.DMA((C, KINDS)),
                pltpu.SemaphoreType.DMA((11,)),
                pltpu.SemaphoreType.DMA((2, 3)),
                pltpu.SemaphoreType.DMA((XS,)),
            ],
            compiler_params=pltpu.CompilerParams(collective_id=0, has_side_effects=True, vmem_limit_bytes=45 * 2**20),
        )(*args)
        return tuple(pl.pallas_call(
            put,
            out_shape=[pltpu.HBM(s, BF) for s in shapes],
            in_specs=[pl.BlockSpec(memory_space=pltpu.VMEM)] * 4,
            out_specs=[pl.BlockSpec(memory_space=pltpu.HBM)] * 4,
            scratch_shapes=[pltpu.SemaphoreType.DMA((4,))],
            compiler_params=pltpu.CompilerParams(vmem_limit_bytes=2**20),
        )(*outs))

    tokens, columns, rows = P("dp", None), P(None, "tp"), P("tp", None)
    return jax.shard_map(
        step,
        mesh=mesh,
        in_specs=(tokens, tokens, P("dp", "tp"), P("dp", "tp"), columns, columns, rows),
        out_specs=(tokens, P("dp", "tp"), P("dp", "tp"), P(("dp", "tp"), None)),
        check_vma=False,
    )
```

time: 181 us -> 99.8 us (0.55)
  Pallas kernels: 0 us -> 98.9 us
  matrix products: 76.6 us -> 0 us
  waiting for transfers between devices: 76.2 us -> 0 us
  local copies, waits for them, and re-layouts: 14 us -> 0 us
  between operations: 14.1 us -> 0.82 us
    pallas_call x0 -> x2, Pallas kernels: none -> 98.9 us  [the longest x1 92.5 us: step(): pl.pallas_call(kernel, out_shape=[pltpu.VMEM(s, BF) for s in shapes], in_...]
    dot_general x6 -> x0, matrix products: 76.6 us -> none  [the longest x1 16.4 us: step(): jnp.dot(d_up, w_up.T, preferred_element_type=jnp.float32)]
    psum x1 -> x0, waiting for transfers between devices: 76.1 us -> none  [step(): dx = lax.psum(term.astype(jnp.bfloat16), 'tp')]
    unnamed x9 -> x0, local copies, waits for them, and re-layouts: 14 us -> none
  transfers between devices with their start and end apart: 1 -> 0, of which waited for: 1 -> 0; matrix products, arithmetic and copies ran while one was open for 23% -> 0% of each run, Pallas kernels for 0% -> 0%
where the time goes in v1:
time: 99.8 us; the launch traced here: 99.7 us
  Pallas kernels  98.9 us (99%)
    pallas_call x1, Pallas kernels, step(): pl.pallas_call(kernel, out_shape=[pltpu.VMEM(s, BF) for s in shapes], in_...  92.5 us
    pallas_call x1, Pallas kernels, step(): pl.pallas_call(put, out_shape=[pltpu.HBM(s, BF) for s in shapes], in_spec...  6.35 us

profile of v1, /device:TPU:0, one launch (start us, length us, event | category | flops | bytes accessed | tf_op | source)
XLA Modules:
  0.0 99.7 jit_solution(11669000453828635785)
XLA Ops:
  0.6 92.5 %shard_map.102 = (bf16[2048,2048]{1,0:T(8,128)(2,1)S(1)}, bf16[2048,768]{1,0:T(8,128)(2,1)S(1)}, bf16[2048,768]{1,0:T(8,128)(2,1)S(1)}, bf16[768,2048]{1,0:T(8,128)(2,1)S(1)}) custom-call(bf16[2048,2048]{1,0:T(8,128)(2,1)} %x.1, bf16[2048,2048]{1,0:T(8,128)(2,1)} %dy.1, bf16[2048,768]{1,0:T(8,128)(2,1)} %gate.1, bf16[2048,768]{1,0:T(8,128)(2,1)} %up.1, ...), custom_call_target="tpu_custom_call" | custom-call | tf_op jit(solution)/shard_map/pallas_call | solution.py:329
  93.2 6.4 %shard_map.103 = (bf16[2048,2048]{1,0:T(8,128)(2,1)}, bf16[2048,768]{1,0:T(8,128)(2,1)}, bf16[2048,768]{1,0:T(8,128)(2,1)}, bf16[768,2048]{1,0:T(8,128)(2,1)}) custom-call(bf16[2048,2048]{1,0:T(8,128)(2,1)S(1)} %get-tuple-element.8.refs_0_, bf16[2048,768]{1,0:T(8,128)(2,1)S(1)} %get-tuple-element.9.refs_1_, bf16[2048,768]{1,0:T(8,128)(2,1)S(1)} %get-tuple-element.10.refs_2_, ...), custom_call_target="tpu_custom_call" | custom-call | tf_op jit(solution)/shard_map/pallas_call | solution.py:357

commit v2 on v0

v2 whole, which is shorter than its diff:
```python
import jax
import jax.numpy as jnp
from jax import lax
from jax.experimental import pallas as pl
from jax.experimental.pallas import tpu as pltpu
from jax.sharding import PartitionSpec as P

MESH = pl.DeviceIdType.MESH
BF, F32 = jnp.bfloat16, jnp.float32
NT = (((1,), (1,)), ((), ()))
TN = (((0,), (0,)), ((), ()))

ROWS, D, HID = 2048, 2048, 768
R = 256
C = ROWS // R
R2, R4 = R // 2, R // 4
OWN = D // 2
HC = OWN // 2
XB = 256
DB = 512
SS, XS, S1, S2, S3 = 2, 3, 2, 3, 3

D2D, RS1, RS2, AG1, AG2, FIN1, FIN2 = 0, 2, 4, 6, 8, 10, 12
KINDS = 14


def dot(a, b, dims):
    return lax.dot_general(a, b, dims, preferred_element_type=F32)


def al(v, m):
    return pl.multiple_of(v, m)


def kernel(x, dy, gate, up, w_gate, w_up, w_down, dx, dw, dwd,
           dyv, gv, uv, dgu, hid, xv, acc1, acc2, acc3, d2d_s, d2d_r, rs1_s, rs1_r, rs2_s, rs2_r,
           send, recv, lw, lc, lx):
    me = lax.axis_index("tp")
    c, y, xx = me % 2, (me // 2) % 2, me // 4
    partner = {"tp": me + 1 - 2 * c}
    ny = {"tp": me + 2 - 4 * y}
    nx = {"tp": me + 4 - 8 * xx}
    first, second = (xx, y), (y, xx)
    to_first, to_second = (nx, ny), (ny, nx)
    both = (0, 1)
    i32 = jnp.int32

    def load_chunk(k):
        slot = k % 2
        r = pl.ds(al(k * R, R), R)
        return [pltpu.make_async_copy(dy.at[r], dyv.at[r], lc.at[slot, 0]),
                pltpu.make_async_copy(gate.at[r], gv.at[slot], lc.at[slot, 1]),
                pltpu.make_async_copy(up.at[r], uv.at[slot], lc.at[slot, 2])]

    def load_x(j):
        slot = j % XS
        return pltpu.make_async_copy(x.at[:, pl.ds(j * XB, XB)], xv.at[slot], lx.at[slot])

    def load_down(i):
        r = pl.ds(i * 256, 256)
        return pltpu.make_async_copy(w_down.at[r], dwd.at[r], lw.at[i])

    def wrows(own):
        return pl.ds(al((c if own else 1 - c) * OWN, OWN), OWN)

    def load_w(own):
        r = wrows(own)
        return [pltpu.make_async_copy(w_gate.at[r], dw.at[r, pl.ds(0, HID)], lw.at[3 + 2 * own]),
                pltpu.make_async_copy(w_up.at[r], dw.at[r, pl.ds(HID, HID)], lw.at[4 + 2 * own])]

    def start(copies):
        for l in copies:
            l.start()

    def wait(copies):
        for l in copies:
            l.wait()

    def rc(src, dst, k, kind, dev):
        return pltpu.make_async_remote_copy(src, dst, send.at[k, kind], recv.at[k, kind],
                                            device_id=dev, device_id_type=MESH)

    def cols(h):
        return pl.ds(al(c * OWN + h * HC, HC), HC)

    def cp(k, kind, h):
        if kind == D2D:
            return rc(d2d_s.at[k % SS, h], d2d_r.at[k, h], k, kind + h, partner)
        if kind == RS1:
            return rc(rs1_s.at[k, h], rs1_r.at[k, h], k, kind + h, to_first[h])
        if kind == RS2:
            return rc(rs2_s.at[k, h], rs2_r.at[k, h], k, kind + h, to_second[h])
        if kind == AG1:
            b = dx.at[pl.ds(al(k * R + first[h] * R2 + second[h] * R4, R4), R4), cols(h)]
            return rc(b, b, k, kind + h, to_second[h])
        p = (1 - first[h]) if kind == FIN2 else first[h]
        b = dx.at[pl.ds(al(k * R + p * R2, R2), R2), cols(h)]
        return rc(b, b, k, kind + h, to_first[h] if kind == AG2 else partner)

    def go(k, kind, halves=both):
        for h in halves:
            cp(k, kind, h).start()

    def arrived(k, kind, halves=both):
        for h in halves:
            cp(k, kind, h).wait_recv()

    def hidden(k, i):
        r, n = pl.ds(al(k * R, R), R), slice(i * 256, (i + 1) * 256)
        slot = k % 2
        dh = dot(dyv[r, :], dwd[n, :], NT)
        g, u = gv[slot, :, n].astype(F32), uv[slot, :, n].astype(F32)
        s = jax.nn.sigmoid(g)
        silu = g * s
        hid[r, n] = (silu * u).astype(BF)
        dgu[r, HID + i * 256:HID + (i + 1) * 256] = (dh * silu).astype(BF)
        dgu[r, n] = (dh * u * (s + silu * (1.0 - s))).astype(BF)

    def term(k, own, halves=both):
        r = pl.ds(al(k * R, R), R)
        for h in halves:
            w = pl.ds(al((c if own else 1 - c) * OWN + h * HC, HC), HC)
            t = dot(dgu[r, :], dw[w, :], NT)
            if own:
                acc1[k % S1, h] = t
            else:
                d2d_s[k % SS, h] = t.astype(BF)

    def sum1(k, halves=both):
        arrived(k, D2D, halves)
        for h in halves:
            keep, leave = (pl.ds(al(v * R2, R2), R2) for v in (first[h], 1 - first[h]))
            rs1_s[k, h] = (acc1[k % S1, h, leave] + d2d_r[k, h, leave].astype(F32)).astype(BF)
            acc2[k % S2, h] = acc1[k % S1, h, keep] + d2d_r[k, h, keep].astype(F32)
        go(k, RS1, halves)

    def sum2(k):
        arrived(k, RS1)
        for h in both:
            keep, leave = (pl.ds(al(v * R4, R4), R4) for v in (second[h], 1 - second[h]))
            rs2_s[k, h] = (acc2[k % S2, h, leave] + rs1_r[k, h, leave].astype(F32)).astype(BF)
            acc3[k % S3, h] = acc2[k % S2, h, keep] + rs1_r[k, h, keep].astype(F32)
        go(k, RS2)

    def sum3(k):
        arrived(k, RS2)
        for h in both:
            p = first[h] * R2 + second[h] * R4
            dx[pl.ds(al(k * R + p, R4), R4), cols(h)] = (acc3[k % S3, h] + rs2_r[k, h].astype(F32)).astype(BF)
        go(k, AG1)

    def gather2(k):
        arrived(k, AG1)
        go(k, AG2)
        go(k, FIN1)

    def gather3(k):
        arrived(k, AG2)
        go(k, FIN2)

    barrier = pltpu.get_barrier_semaphore()
    for dev in (partner, ny, nx):
        pl.semaphore_signal(barrier, inc=1, device_id=dev, device_id_type=MESH)

    k0 = i32(0)
    load_down(0).start()
    start(load_chunk(k0))
    load_down(1).start()
    load_down(2).start()
    load_down(0).wait()
    wait(load_chunk(k0))
    start(load_w(0))
    load_down(1).wait()
    load_down(2).wait()
    start(load_w(1))
    for i in range(3):
        hidden(k0, i)
    start(load_chunk(i32(1)))
    wait(load_w(0))
    pl.semaphore_wait(barrier, 3)
    for h in both:
        term(k0, 0, (h,))
        go(k0, D2D, (h,))
    wait(load_w(1))
    for h in both:
        term(k0, 1, (h,))
        sum1(k0, (h,))
    for j in range(XS):
        load_x(j).start()

    @pl.loop(1, C)
    def _(k):
        @pl.when(k >= 3)
        def _():
            sum2(k - 3)

        @pl.when(k >= 5)
        def _():
            sum3(k - 5)

        wait(load_chunk(k))

        @pl.when(k + 1 < C)
        def _():
            start(load_chunk(k + 1))

        for i in range(3):
            hidden(k, i)

        @pl.when(k >= 2)
        def _():
            sum1(k - 1)
            for h in both:
                cp(k - 2, D2D, h).wait_send()

        term(k, 0)
        go(k, D2D)
        term(k, 1)

    def piece_x(j):
        load_x(j).wait()
        dw[j * XB:(j + 1) * XB, :] = dot(xv[j % XS], dgu[...], TN).astype(BF)
        if j + XS < D // XB:
            load_x(j + XS).start()

    def piece_y(j):
        n = slice(j * DB, (j + 1) * DB)
        dwd[:, n] = dot(hid[...], dyv[:, n], TN).astype(BF)

    pieces = []
    for j in range(4):
        pieces += [lambda j=j: piece_x(2 * j), lambda j=j: piece_x(2 * j + 1), lambda j=j: piece_y(j)]
    events = {
        0: [(sum1, 7)],
        1: [(sum2, 5)],
        2: [(sum3, 3)],
        3: [(sum2, 6), (gather2, 0)],
        4: [(sum3, 4), (gather2, 1)],
        5: [(sum2, 7), (sum3, 5), (gather2, 2)],
        6: [(sum3, 6), (gather2, 3)],
        7: [(sum3, 7)],
        8: [(gather2, 4)],
        9: [(gather2, 5), (gather3, 0)],
        10: [(gather2, 6), (gather3, 1)],
        11: [(gather2, 7), (gather3, 2)],
    }
    for i, piece in enumerate(pieces):
        for f, k in events[i]:
            f(i32(k))
        piece()
    for k in range(3, C):
        gather3(i32(k))

    @pl.loop(0, C)
    def _(k):
        @pl.when(k >= C - SS)
        def _():
            for h in both:
                cp(k, D2D, h).wait_send()

        for h in both:
            for kind in (RS1, RS2, AG1, AG2):
                cp(k, kind, h).wait_send()
            for kind in (FIN1, FIN2):
                cp(k, kind, h).wait()


def put(dx, dw, dwd, o_dx, o_gate, o_up, o_down, sem):
    copies = [pltpu.make_async_copy(dx, o_dx, sem.at[0]),
              pltpu.make_async_copy(dw.at[:, pl.ds(0, HID)], o_gate, sem.at[1]),
              pltpu.make_async_copy(dw.at[:, pl.ds(HID, HID)], o_up, sem.at[2]),
              pltpu.make_async_copy(dwd, o_down, sem.at[3])]
    for c in copies:
        c.start()
    for c in copies:
        c.wait()


def solution(mesh):
    def step(*args):
        outs = pl.pallas_call(
            kernel,
            out_shape=[pltpu.VMEM((ROWS, D), BF), pltpu.VMEM((D, 2 * HID), BF), pltpu.VMEM((HID, D), BF)],
            in_specs=[pl.BlockSpec(memory_space=pltpu.HBM)] * 7,
            out_specs=[pl.BlockSpec(memory_space=pltpu.VMEM)] * 3,
            scratch_shapes=[
                pltpu.VMEM((ROWS, D), BF),
                pltpu.VMEM((2, R, HID), BF),
                pltpu.VMEM((2, R, HID), BF),
                pltpu.VMEM((ROWS, 2 * HID), BF),
                pltpu.VMEM((ROWS, HID), BF),
                pltpu.VMEM((XS, ROWS, XB), BF),
                pltpu.VMEM((S1, 2, R, HC), F32),
                pltpu.VMEM((S2, 2, R2, HC), F32),
                pltpu.VMEM((S3, 2, R4, HC), F32),
                pltpu.VMEM((SS, 2, R, HC), BF),
                pltpu.VMEM((C, 2, R, HC), BF),
                pltpu.VMEM((C, 2, R2, HC), BF),
                pltpu.VMEM((C, 2, R2, HC), BF),
                pltpu.VMEM((C, 2, R4, HC), BF),
                pltpu.VMEM((C, 2, R4, HC), BF),
                pltpu.SemaphoreType.DMA((C, KINDS)),
                pltpu.SemaphoreType.DMA((C, KINDS)),
                pltpu.SemaphoreType.DMA((7,)),
                pltpu.SemaphoreType.DMA((2, 3)),
                pltpu.SemaphoreType.DMA((XS,)),
            ],
            compiler_params=pltpu.CompilerParams(collective_id=0, has_side_effects=True, vmem_limit_bytes=45 * 2**20),
        )(*args)
        shapes = [(ROWS, D), (D, HID), (D, HID), (HID, D)]
        return tuple(pl.pallas_call(
            put,
            out_shape=[pltpu.HBM(s, BF) for s in shapes],
            in_specs=[pl.BlockSpec(memory_space=pltpu.VMEM)] * 3,
            out_specs=[pl.BlockSpec(memory_space=pltpu.HBM)] * 4,
            scratch_shapes=[pltpu.SemaphoreType.DMA((4,))],
            compiler_params=pltpu.CompilerParams(vmem_limit_bytes=2**20),
        )(*outs))

    tokens, columns, rows = P("dp", None), P(None, "tp"), P("tp", None)
    return jax.shard_map(
        step,
        mesh=mesh,
        in_specs=(tokens, tokens, P("dp", "tp"), P("dp", "tp"), columns, columns, rows),
        out_specs=(tokens, P("dp", "tp"), P("dp", "tp"), P(("dp", "tp"), None)),
        check_vma=False,
    )
```

time: 181 us -> 92.2 us (0.51)
  Pallas kernels: 0 us -> 91.3 us
  matrix products: 76.6 us -> 0 us
  waiting for transfers between devices: 76.2 us -> 0 us
  local copies, waits for them, and re-layouts: 14 us -> 0 us
  between operations: 14.1 us -> 0.82 us
    pallas_call x0 -> x2, Pallas kernels: none -> 91.3 us  [the longest x1 84.9 us: step(): pl.pallas_call(kernel, out_shape=[pltpu.VMEM((ROWS, D), BF), pltpu.VMEM((...]
    dot_general x6 -> x0, matrix products: 76.6 us -> none  [the longest x1 16.4 us: step(): jnp.dot(d_up, w_up.T, preferred_element_type=jnp.float32)]
    psum x1 -> x0, waiting for transfers between devices: 76.1 us -> none  [step(): dx = lax.psum(term.astype(jnp.bfloat16), 'tp')]
    unnamed x9 -> x0, local copies, waits for them, and re-layouts: 14 us -> none
  transfers between devices with their start and end apart: 1 -> 0, of which waited for: 1 -> 0; matrix products, arithmetic and copies ran while one was open for 23% -> 0% of each run, Pallas kernels for 0% -> 0%
where the time goes in v2:
time: 92.2 us; the launch traced here: 92.1 us
  Pallas kernels  91.3 us (99%)
    pallas_call x1, Pallas kernels, step(): pl.pallas_call(kernel, out_shape=[pltpu.VMEM((ROWS, D), BF), pltpu.VMEM((...  84.9 us
    pallas_call x1, Pallas kernels, step(): pl.pallas_call(put, out_shape=[pltpu.HBM(s, BF) for s in shapes], in_spec...  6.35 us

profile of v2, /device:TPU:0, one launch (start us, length us, event | category | flops | bytes accessed | tf_op | source)
XLA Modules:
  0.0 92.1 jit_solution(5897860357828513655)
XLA Ops:
  0.6 84.9 %shard_map.102 = (bf16[2048,2048]{1,0:T(8,128)(2,1)S(1)}, bf16[2048,1536]{1,0:T(8,128)(2,1)S(1)}, bf16[768,2048]{1,0:T(8,128)(2,1)S(1)}) custom-call(bf16[2048,2048]{1,0:T(8,128)(2,1)} %x.1, bf16[2048,2048]{1,0:T(8,128)(2,1)} %dy.1, bf16[2048,768]{1,0:T(8,128)(2,1)} %gate.1, bf16[2048,768]{1,0:T(8,128)(2,1)} %up.1, bf16[2048,768]{1,0:T(8,128)(2,1)} %w_gate.1, ...), custom_call_target="tpu_custom_call" | custom-call | tf_op jit(solution)/shard_map/pallas_call | solution.py:281
  85.5 6.4 %shard_map.103 = (bf16[2048,2048]{1,0:T(8,128)(2,1)}, bf16[2048,768]{1,0:T(8,128)(2,1)}, bf16[2048,768]{1,0:T(8,128)(2,1)}, bf16[768,2048]{1,0:T(8,128)(2,1)}) custom-call(bf16[2048,2048]{1,0:T(8,128)(2,1)S(1)} %get-tuple-element.7.dx, bf16[2048,1536]{1,0:T(8,128)(2,1)S(1)} %get-tuple-element.8.dw, bf16[768,2048]{1,0:T(8,128)(2,1)S(1)} %get-tuple-element.9.dwd), custom_call_target="tpu_custom_call" | custom-call | tf_op jit(solution)/shard_map/pallas_call | solution.py:311

commit v3 on v2

--- a/solution.py
+++ b/solution.py
@@ -20,8 +20,7 @@
 DB = 512
 SS, XS, S1, S2, S3 = 2, 3, 2, 3, 3
 
-D2D, RS1, RS2, AG1, AG2, FIN1, FIN2 = 0, 2, 4, 6, 8, 10, 12
-KINDS = 14
+D2D, RS1, RS2, AG1, AG2, FIN1, FIN2 = range(7)
 
 
 def dot(a, b, dims):
@@ -33,8 +32,8 @@
 
 
 def kernel(x, dy, gate, up, w_gate, w_up, w_down, dx, dw, dwd,
-           dyv, gv, uv, dgu, hid, xv, acc1, acc2, acc3, d2d_s, d2d_r, rs1_s, rs1_r, rs2_s, rs2_r,
-           send, recv, lw, lc, lx):
+           dyv, gv, uv, dgu, hid, st0, st1, xv, acc1, acc2, acc3, d2d_s, d2d_r, rs1_s, rs1_r, rs2_s, rs2_r,
+           send, recv, fin, lw, lc, lx):
     me = lax.axis_index("tp")
     c, y, xx = me % 2, (me // 2) % 2, me // 4
     partner = {"tp": me + 1 - 2 * c}
@@ -76,63 +75,80 @@
         for l in copies:
             l.wait()
 
-    def rc(src, dst, k, kind, dev):
-        return pltpu.make_async_remote_copy(src, dst, send.at[k, kind], recv.at[k, kind],
+    def rc(src, dst, kind, sem, dev, slot=0):
+        return pltpu.make_async_remote_copy(src, dst, send.at[7 + slot if kind == D2D else kind], sem,
                                             device_id=dev, device_id_type=MESH)
 
     def cols(h):
         return pl.ds(al(c * OWN + h * HC, HC), HC)
 
-    def cp(k, kind, h):
+    def cp(k, kind, h, first_chunk=False):
+        sem = fin.at[kind - FIN1] if kind >= FIN1 else recv.at[C if first_chunk and h else k, kind]
         if kind == D2D:
-            return rc(d2d_s.at[k % SS, h], d2d_r.at[k, h], k, kind + h, partner)
+            return rc(d2d_s.at[k % SS, h], d2d_r.at[k, h], kind, sem, partner, k % SS)
         if kind == RS1:
-            return rc(rs1_s.at[k, h], rs1_r.at[k, h], k, kind + h, to_first[h])
+            return rc(rs1_s.at[k, h], rs1_r.at[k, h], kind, sem, to_first[h])
         if kind == RS2:
-            return rc(rs2_s.at[k, h], rs2_r.at[k, h], k, kind + h, to_second[h])
+            return rc(rs2_s.at[k, h], rs2_r.at[k, h], kind, sem, to_second[h])
         if kind == AG1:
             b = dx.at[pl.ds(al(k * R + first[h] * R2 + second[h] * R4, R4), R4), cols(h)]
-            return rc(b, b, k, kind + h, to_second[h])
+            return rc(b, b, kind, sem, to_second[h])
         p = (1 - first[h]) if kind == FIN2 else first[h]
         b = dx.at[pl.ds(al(k * R + p * R2, R2), R2), cols(h)]
-        return rc(b, b, k, kind + h, to_first[h] if kind == AG2 else partner)
-
-    def go(k, kind, halves=both):
+        return rc(b, b, kind, sem, to_first[h] if kind == AG2 else partner)
+
+    def go(k, kind):
+        for h in both:
+            cp(k, kind, h).start()
+
+    sizes = {D2D: d2d_r, RS1: rs1_r, RS2: rs2_r, AG1: rs2_r, AG2: rs1_r, FIN1: rs1_r, FIN2: rs1_r}
+
+    def sent(slot):
+        rc(d2d_s.at[slot], d2d_r.at[0], D2D, fin.at[0], partner, slot).wait_send()
+
+    def arrived(k, kind):
+        b = sizes[kind].at[k]
+        rc(b, b, kind, recv.at[k, kind], partner).wait_recv()
+
+    stage = (st0, st1)
+
+    def hidden(k, slot):
+        r = pl.ds(al(k * R, R), R)
+        st = stage[slot]
+        dh = dot(dyv[r, :], dwd[...], NT)
+        for i in range(3):
+            n = slice(i * 256, (i + 1) * 256)
+            g, u, d = gv[slot, :, n].astype(F32), uv[slot, :, n].astype(F32), dh[:, n]
+            s = jax.nn.sigmoid(g)
+            silu = g * s
+            hid[r, n] = (silu * u).astype(BF)
+            m = slice(HID + i * 256, HID + (i + 1) * 256)
+            d_up = (d * silu).astype(BF)
+            d_gate = (d * u * (s + silu * (1.0 - s))).astype(BF)
+            st[:, m], dgu[r, m] = d_up, d_up
+            st[:, n], dgu[r, n] = d_gate, d_gate
+
+    def term(k, slot, own, halves=both):
+        n = HC * len(halves)
+        w = pl.ds(al((c if own else 1 - c) * OWN + halves[0] * HC, HC), n)
+        t = dot(stage[slot][...], dw[w, :], NT)
         for h in halves:
-            cp(k, kind, h).start()
-
-    def arrived(k, kind, halves=both):
-        for h in halves:
-            cp(k, kind, h).wait_recv()
-
-    def hidden(k, i):
-        r, n = pl.ds(al(k * R, R), R), slice(i * 256, (i + 1) * 256)
-        slot = k % 2
-        dh = dot(dyv[r, :], dwd[n, :], NT)
-        g, u = gv[slot, :, n].astype(F32), uv[slot, :, n].astype(F32)
-        s = jax.nn.sigmoid(g)
-        silu = g * s
-        hid[r, n] = (silu * u).astype(BF)
-        dgu[r, HID + i * 256:HID + (i + 1) * 256] = (dh * silu).astype(BF)
-        dgu[r, n] = (dh * u * (s + silu * (1.0 - s))).astype(BF)
-
-    def term(k, own, halves=both):
-        r = pl.ds(al(k * R, R), R)
-        for h in halves:
-            w = pl.ds(al((c if own else 1 - c) * OWN + h * HC, HC), HC)
-            t = dot(dgu[r, :], dw[w, :], NT)
+            part = t[:, (h - halves[0]) * HC:(h - halves[0] + 1) * HC]
             if own:
-                acc1[k % S1, h] = t
+                acc1[slot, h] = part
             else:
-                d2d_s[k % SS, h] = t.astype(BF)
-
-    def sum1(k, halves=both):
-        arrived(k, D2D, halves)
-        for h in halves:
-            keep, leave = (pl.ds(al(v * R2, R2), R2) for v in (first[h], 1 - first[h]))
-            rs1_s[k, h] = (acc1[k % S1, h, leave] + d2d_r[k, h, leave].astype(F32)).astype(BF)
-            acc2[k % S2, h] = acc1[k % S1, h, keep] + d2d_r[k, h, keep].astype(F32)
-        go(k, RS1, halves)
+                d2d_s[slot, h] = part.astype(BF)
+
+    def add1(k, h):
+        keep, leave = (pl.ds(al(v * R2, R2), R2) for v in (first[h], 1 - first[h]))
+        rs1_s[k, h] = (acc1[k % S1, h, leave] + d2d_r[k, h, leave].astype(F32)).astype(BF)
+        acc2[k % S2, h] = acc1[k % S1, h, keep] + d2d_r[k, h, keep].astype(F32)
+
+    def sum1(k):
+        arrived(k, D2D)
+        for h in both:
+            add1(k, h)
+        go(k, RS1)
 
     def sum2(k):
         arrived(k, RS1)
@@ -163,34 +179,45 @@
         pl.semaphore_signal(barrier, inc=1, device_id=dev, device_id_type=MESH)
 
     k0 = i32(0)
-    load_down(0).start()
-    start(load_chunk(k0))
-    load_down(1).start()
-    load_down(2).start()
-    load_down(0).wait()
-    wait(load_chunk(k0))
+    chunk0 = load_chunk(k0)
+    for i in range(3):
+        load_down(i).start()
+        chunk0[i].start()
     start(load_w(0))
-    load_down(1).wait()
-    load_down(2).wait()
     start(load_w(1))
+    start(load_chunk(i32(1)))
     for i in range(3):
-        hidden(k0, i)
-    start(load_chunk(i32(1)))
+        load_down(i).wait()
+    wait(chunk0)
+    hidden(k0, 0)
     wait(load_w(0))
     pl.semaphore_wait(barrier, 3)
+    term(k0, 0, 0)
     for h in both:
-        term(k0, 0, (h,))
-        go(k0, D2D, (h,))
+        cp(k0, D2D, h, True).start()
     wait(load_w(1))
+    wait(load_chunk(i32(1)))
+    start(load_chunk(i32(2)))
+    hidden(i32(1), 1)
+    term(k0, 0, 1)
     for h in both:
-        term(k0, 1, (h,))
-        sum1(k0, (h,))
+        cp(k0, D2D, h, True).wait_recv()
+        add1(k0, h)
+        cp(k0, RS1, h).start()
     for j in range(XS):
         load_x(j).start()
 
-    @pl.loop(1, C)
-    def _(k):
-        @pl.when(k >= 3)
+    def step(k, slot, last=False):
+        if not last:
+            @pl.when(k + 2 < C)
+            def _():
+                start(load_chunk(k + 2))
+
+        @pl.when(k >= 2)
+        def _():
+            sum1(k - 1)
+
+        @pl.when(k >= 4)
         def _():
             sum2(k - 3)
 
@@ -198,24 +225,28 @@
         def _():
             sum3(k - 5)
 
-        wait(load_chunk(k))
-
-        @pl.when(k + 1 < C)
-        def _():
-            start(load_chunk(k + 1))
-
-        for i in range(3):
-            hidden(k, i)
-
         @pl.when(k >= 2)
         def _():
-            sum1(k - 1)
-            for h in both:
-                cp(k - 2, D2D, h).wait_send()
-
-        term(k, 0)
+            sent(slot)
+
+        term(k, slot, 0)
         go(k, D2D)
-        term(k, 1)
+        if slot == 0:
+            @pl.when(k == 2)
+            def _():
+                sum2(i32(0))
+
+        if not last:
+            wait(load_chunk(k + 1))
+            hidden(k + 1, 1 - slot)
+        term(k, slot, 1)
+
+    @pl.loop(0, C // 2 - 1)
+    def _(i):
+        step(2 * i + 1, 1)
+        step(2 * i + 2, 0)
+
+    step(i32(C - 1), 1, last=True)
 
     def piece_x(j):
         load_x(j).wait()
@@ -234,35 +265,31 @@
         0: [(sum1, 7)],
         1: [(sum2, 5)],
         2: [(sum3, 3)],
-        3: [(sum2, 6), (gather2, 0)],
-        4: [(sum3, 4), (gather2, 1)],
-        5: [(sum2, 7), (sum3, 5), (gather2, 2)],
-        6: [(sum3, 6), (gather2, 3)],
-        7: [(sum3, 7)],
-        8: [(gather2, 4)],
-        9: [(gather2, 5), (gather3, 0)],
-        10: [(gather2, 6), (gather3, 1)],
-        11: [(gather2, 7), (gather3, 2)],
+        3: [(sum2, 6)],
+        4: [(sum3, 4), (gather2, 0)],
+        5: [(gather2, 1)],
+        6: [(sum2, 7), (gather2, 2)],
+        7: [(sum3, 5)],
+        8: [(sum3, 6), (gather2, 3)],
+        9: [(gather2, 4), (gather3, 0)],
+        10: [(sum3, 7)],
+        11: [(gather2, 5), (gather3, 1)],
     }
     for i, piece in enumerate(pieces):
         for f, k in events[i]:
             f(i32(k))
         piece()
-    for k in range(3, C):
-        gather3(i32(k))
-
-    @pl.loop(0, C)
-    def _(k):
-        @pl.when(k >= C - SS)
-        def _():
-            for h in both:
-                cp(k, D2D, h).wait_send()
-
-        for h in both:
-            for kind in (RS1, RS2, AG1, AG2):
-                cp(k, kind, h).wait_send()
-            for kind in (FIN1, FIN2):
-                cp(k, kind, h).wait()
+    for f, k in [(gather2, 6), (gather3, 2), (gather3, 3), (gather3, 4), (gather2, 7), (gather3, 5), (gather3, 6), (gather3, 7)]:
+        f(i32(k))
+
+    for kind, b in sizes.items():
+        w = rc(b, b, kind, fin.at[max(kind - FIN1, 0)], partner)
+        if kind >= FIN1:
+            w.wait_recv()
+        if kind != D2D:
+            w.wait_send()
+    for slot in range(SS):
+        sent(slot)
 
 
 def put(dx, dw, dwd, o_dx, o_gate, o_up, o_down, sem):
@@ -289,6 +316,8 @@
                 pltpu.VMEM((2, R, HID), BF),
                 pltpu.VMEM((ROWS, 2 * HID), BF),
                 pltpu.VMEM((ROWS, HID), BF),
+                pltpu.VMEM((R, 2 * HID), BF),
+                pltpu.VMEM((R, 2 * HID), BF),
                 pltpu.VMEM((XS, ROWS, XB), BF),
                 pltpu.VMEM((S1, 2, R, HC), F32),
                 pltpu.VMEM((S2, 2, R2, HC), F32),
@@ -299,13 +328,14 @@
                 pltpu.VMEM((C, 2, R2, HC), BF),
                 pltpu.VMEM((C, 2, R4, HC), BF),
                 pltpu.VMEM((C, 2, R4, HC), BF),
-                pltpu.SemaphoreType.DMA((C, KINDS)),
-                pltpu.SemaphoreType.DMA((C, KINDS)),
+                pltpu.SemaphoreType.DMA((7 + SS,)),
+                pltpu.SemaphoreType.DMA((C + 1, 5)),
+                pltpu.SemaphoreType.DMA((2,)),
                 pltpu.SemaphoreType.DMA((7,)),
                 pltpu.SemaphoreType.DMA((2, 3)),
                 pltpu.SemaphoreType.DMA((XS,)),
             ],
-            compiler_params=pltpu.CompilerParams(collective_id=0, has_side_effects=True, vmem_limit_bytes=45 * 2**20),
+            compiler_params=pltpu.CompilerParams(collective_id=0, has_side_effects=True, vmem_limit_bytes=46 * 2**20),
         )(*args)
         shapes = [(ROWS, D), (D, HID), (D, HID), (HID, D)]
         return tuple(pl.pallas_call(

time: 92.2 us -> 88.6 us (0.961)
  Pallas kernels: 91.3 us -> 87.7 us
    pallas_call x1, Pallas kernels: 84.9 us -> 81.3 us  [step(): pl.pallas_call(kernel, out_shape=[pltpu.VMEM((ROWS, D), BF), pltpu.VMEM((...]
where the time goes in v3:
time: 88.6 us; the launch traced here: 88.5 us
  Pallas kernels  87.7 us (99%)
    pallas_call x1, Pallas kernels, step(): pl.pallas_call(kernel, out_shape=[pltpu.VMEM((ROWS, D), BF), pltpu.VMEM((...  81.3 us
    pallas_call x1, Pallas kernels, step(): pl.pallas_call(put, out_shape=[pltpu.HBM(s, BF) for s in shapes], in_spec...  6.35 us

profile of v3, /device:TPU:0, one launch (start us, length us, event | category | flops | bytes accessed | tf_op | source)
XLA Modules:
  0.0 88.5 jit_solution(628326298541416664)
XLA Ops:
  0.6 81.3 %shard_map.102 = (bf16[2048,2048]{1,0:T(8,128)(2,1)S(1)}, bf16[2048,1536]{1,0:T(8,128)(2,1)S(1)}, bf16[768,2048]{1,0:T(8,128)(2,1)S(1)}) custom-call(bf16[2048,2048]{1,0:T(8,128)(2,1)} %x.1, bf16[2048,2048]{1,0:T(8,128)(2,1)} %dy.1, bf16[2048,768]{1,0:T(8,128)(2,1)} %gate.1, bf16[2048,768]{1,0:T(8,128)(2,1)} %up.1, bf16[2048,768]{1,0:T(8,128)(2,1)} %w_gate.1, ...), custom_call_target="tpu_custom_call" | custom-call | tf_op jit(solution)/shard_map/pallas_call | solution.py:308
  82.0 6.4 %shard_map.103 = (bf16[2048,2048]{1,0:T(8,128)(2,1)}, bf16[2048,768]{1,0:T(8,128)(2,1)}, bf16[2048,768]{1,0:T(8,128)(2,1)}, bf16[768,2048]{1,0:T(8,128)(2,1)}) custom-call(bf16[2048,2048]{1,0:T(8,128)(2,1)S(1)} %get-tuple-element.7.dx, bf16[2048,1536]{1,0:T(8,128)(2,1)S(1)} %get-tuple-element.8.dw, bf16[768,2048]{1,0:T(8,128)(2,1)S(1)} %get-tuple-element.9.dwd), custom_call_target="tpu_custom_call" | custom-call | tf_op jit(solution)/shard_map/pallas_call | solution.py:341

commit v4 on v3

--- a/solution.py
+++ b/solution.py
@@ -229,8 +229,9 @@
         def _():
             sent(slot)
 
-        term(k, slot, 0)
-        go(k, D2D)
+        for h in both:
+            term(k, slot, 0, (h,))
+            cp(k, D2D, h).start()
         if slot == 0:
             @pl.when(k == 2)
             def _():
@@ -293,12 +294,23 @@
 
 
 def put(dx, dw, dwd, o_dx, o_gate, o_up, o_down, sem):
-    copies = [pltpu.make_async_copy(dx, o_dx, sem.at[0]),
-              pltpu.make_async_copy(dw.at[:, pl.ds(0, HID)], o_gate, sem.at[1]),
-              pltpu.make_async_copy(dw.at[:, pl.ds(HID, HID)], o_up, sem.at[2]),
-              pltpu.make_async_copy(dwd, o_down, sem.at[3])]
-    for c in copies:
-        c.start()
+    copies = []
+
+    def add(a, b):
+        copies.append(pltpu.make_async_copy(a, b, sem.at[len(copies)]))
+
+    for i in range(4):
+        n = ROWS // 4
+        r = pl.ds(i * n, n)
+        add(dx.at[r], o_dx.at[r])
+        add(dw.at[r, pl.ds(0, HID)], o_gate.at[r])
+        add(dw.at[r, pl.ds(HID, HID)], o_up.at[r])
+        if i < 4:
+            n = HID // 4
+            r = pl.ds(i * n, n)
+            add(dwd.at[r], o_down.at[r])
+    for i, c in enumerate(copies):
+        c.start(priority=i % 2 if False else 0)
     for c in copies:
         c.wait()
 
@@ -343,7 +355,7 @@
             out_shape=[pltpu.HBM(s, BF) for s in shapes],
             in_specs=[pl.BlockSpec(memory_space=pltpu.VMEM)] * 3,
             out_specs=[pl.BlockSpec(memory_space=pltpu.HBM)] * 4,
-            scratch_shapes=[pltpu.SemaphoreType.DMA((4,))],
+            scratch_shapes=[pltpu.SemaphoreType.DMA((16,))],
             compiler_params=pltpu.CompilerParams(vmem_limit_bytes=2**20),
         )(*outs))
 

time: 88.6 us -> 88.4 us (level)
  no operation moved by 1% of the time
where the time goes in v4:
time: 88.4 us
  Pallas kernels  87.5 us (99%)
    pallas_call x1, Pallas kernels, step(): pl.pallas_call(kernel, out_shape=[pltpu.VMEM((ROWS, D), BF), pltpu.VMEM((...  81.3 us
    pallas_call x1, Pallas kernels, step(): pl.pallas_call(put, out_shape=[pltpu.HBM(s, BF) for s in shapes], in_spec...  6.27 us

profile of v4, /device:TPU:0, one launch (start us, length us, event | category | flops | bytes accessed | tf_op | source)
XLA Modules:
  0.0 88.4 jit_solution(16401263802896704803)
XLA Ops:
  0.6 81.3 %shard_map.102 = (bf16[2048,2048]{1,0:T(8,128)(2,1)S(1)}, bf16[2048,1536]{1,0:T(8,128)(2,1)S(1)}, bf16[768,2048]{1,0:T(8,128)(2,1)S(1)}) custom-call(bf16[2048,2048]{1,0:T(8,128)(2,1)} %x.1, bf16[2048,2048]{1,0:T(8,128)(2,1)} %dy.1, bf16[2048,768]{1,0:T(8,128)(2,1)} %gate.1, bf16[2048,768]{1,0:T(8,128)(2,1)} %up.1, bf16[2048,768]{1,0:T(8,128)(2,1)} %w_gate.1, ...), custom_call_target="tpu_custom_call" | custom-call | tf_op jit(solution)/shard_map/pallas_call | solution.py:320
  81.9 6.3 %shard_map.103 = (bf16[2048,2048]{1,0:T(8,128)(2,1)}, bf16[2048,768]{1,0:T(8,128)(2,1)}, bf16[2048,768]{1,0:T(8,128)(2,1)}, bf16[768,2048]{1,0:T(8,128)(2,1)}) custom-call(bf16[2048,2048]{1,0:T(8,128)(2,1)S(1)} %get-tuple-element.7.dx, bf16[2048,1536]{1,0:T(8,128)(2,1)S(1)} %get-tuple-element.8.dw, bf16[768,2048]{1,0:T(8,128)(2,1)S(1)} %get-tuple-element.9.dwd), custom_call_target="tpu_custom_call" | custom-call | tf_op jit(solution)/shard_map/pallas_call | solution.py:353

commit v5 on v4

--- a/solution.py
+++ b/solution.py
@@ -55,9 +55,10 @@
         slot = j % XS
         return pltpu.make_async_copy(x.at[:, pl.ds(j * XB, XB)], xv.at[slot], lx.at[slot])
 
-    def load_down(i):
-        r = pl.ds(i * 256, 256)
-        return pltpu.make_async_copy(w_down.at[r], dwd.at[r], lw.at[i])
+    def load_half(i):
+        n, r = pl.ds(i * OWN, OWN), pl.ds(0, R)
+        return [pltpu.make_async_copy(dy.at[r, n], dyv.at[r, n], lw.at[i]),
+                pltpu.make_async_copy(w_down.at[:, n], dwd.at[:, n], lw.at[7 + i])]
 
     def wrows(own):
         return pl.ds(al((c if own else 1 - c) * OWN, OWN), OWN)
@@ -113,9 +114,11 @@
     stage = (st0, st1)
 
     def hidden(k, slot):
+        hidden2(k, slot, dot(dyv[pl.ds(al(k * R, R), R), :], dwd[...], NT))
+
+    def hidden2(k, slot, dh):
         r = pl.ds(al(k * R, R), R)
         st = stage[slot]
-        dh = dot(dyv[r, :], dwd[...], NT)
         for i in range(3):
             n = slice(i * 256, (i + 1) * 256)
             g, u, d = gv[slot, :, n].astype(F32), uv[slot, :, n].astype(F32), dh[:, n]
@@ -179,17 +182,21 @@
         pl.semaphore_signal(barrier, inc=1, device_id=dev, device_id_type=MESH)
 
     k0 = i32(0)
-    chunk0 = load_chunk(k0)
-    for i in range(3):
-        load_down(i).start()
-        chunk0[i].start()
+    chunk0 = load_chunk(k0)[1:]
+    start(load_half(0))
+    start(load_half(1))
+    start(chunk0)
     start(load_w(0))
     start(load_w(1))
     start(load_chunk(i32(1)))
-    for i in range(3):
-        load_down(i).wait()
+    wait(load_half(0))
+    left = dot(dyv[:R, :OWN], dwd[:, :OWN], NT)
+    acc1[1, 0] = left[:, :HC]
+    acc1[1, 1, :, :HID - HC] = left[:, HC:]
+    wait(load_half(1))
     wait(chunk0)
-    hidden(k0, 0)
+    left = jnp.concatenate([acc1[1, 0], acc1[1, 1, :, :HID - HC]], axis=1)
+    hidden2(k0, 0, left + dot(dyv[:R, OWN:], dwd[:, OWN:], NT))
     wait(load_w(0))
     pl.semaphore_wait(barrier, 3)
     term(k0, 0, 0)
@@ -343,7 +350,7 @@
                 pltpu.SemaphoreType.DMA((7 + SS,)),
                 pltpu.SemaphoreType.DMA((C + 1, 5)),
                 pltpu.SemaphoreType.DMA((2,)),
-                pltpu.SemaphoreType.DMA((7,)),
+                pltpu.SemaphoreType.DMA((9,)),
                 pltpu.SemaphoreType.DMA((2, 3)),
                 pltpu.SemaphoreType.DMA((XS,)),
             ],

time: 88.4 us -> 88 us (level)
  no operation moved by 1% of the time
where the time goes in v5:
time: 88 us; the launch traced here: 87.9 us
  Pallas kernels  87.1 us (99%)
    pallas_call x1, Pallas kernels, step(): pl.pallas_call(kernel, out_shape=[pltpu.VMEM((ROWS, D), BF), pltpu.VMEM((...  80.8 us
    pallas_call x1, Pallas kernels, step(): pl.pallas_call(put, out_shape=[pltpu.HBM(s, BF) for s in shapes], in_spec...  6.27 us

profile of v5, /device:TPU:0, one launch (start us, length us, event | category | flops | bytes accessed | tf_op | source)
XLA Modules:
  0.0 87.9 jit_solution(8567249427341482056)
XLA Ops:
  0.6 80.8 %shard_map.102 = (bf16[2048,2048]{1,0:T(8,128)(2,1)S(1)}, bf16[2048,1536]{1,0:T(8,128)(2,1)S(1)}, bf16[768,2048]{1,0:T(8,128)(2,1)S(1)}) custom-call(bf16[2048,2048]{1,0:T(8,128)(2,1)} %x.1, bf16[2048,2048]{1,0:T(8,128)(2,1)} %dy.1, bf16[2048,768]{1,0:T(8,128)(2,1)} %gate.1, bf16[2048,768]{1,0:T(8,128)(2,1)} %up.1, bf16[2048,768]{1,0:T(8,128)(2,1)} %w_gate.1, ...), custom_call_target="tpu_custom_call" | custom-call | tf_op jit(solution)/shard_map/pallas_call | solution.py:327
  81.5 6.3 %shard_map.103 = (bf16[2048,2048]{1,0:T(8,128)(2,1)}, bf16[2048,768]{1,0:T(8,128)(2,1)}, bf16[2048,768]{1,0:T(8,128)(2,1)}, bf16[768,2048]{1,0:T(8,128)(2,1)}) custom-call(bf16[2048,2048]{1,0:T(8,128)(2,1)S(1)} %get-tuple-element.7.dx, bf16[2048,1536]{1,0:T(8,128)(2,1)S(1)} %get-tuple-element.8.dw, bf16[768,2048]{1,0:T(8,128)(2,1)S(1)} %get-tuple-element.9.dwd), custom_call_target="tpu_custom_call" | custom-call | tf_op jit(solution)/shard_map/pallas_call | solution.py:360

commit v6 on v5

--- a/solution.py
+++ b/solution.py
@@ -18,6 +18,7 @@
 HC = OWN // 2
 XB = 256
 DB = 512
+RT = 16
 SS, XS, S1, S2, S3 = 2, 3, 2, 3, 3
 
 D2D, RS1, RS2, AG1, AG2, FIN1, FIN2 = range(7)
@@ -33,7 +34,7 @@
 
 def kernel(x, dy, gate, up, w_gate, w_up, w_down, dx, dw, dwd,
            dyv, gv, uv, dgu, hid, st0, st1, xv, acc1, acc2, acc3, d2d_s, d2d_r, rs1_s, rs1_r, rs2_s, rs2_r,
-           send, recv, fin, lw, lc, lx):
+           send, recv, fin, last, lw, lc, lx):
     me = lax.axis_index("tp")
     c, y, xx = me % 2, (me // 2) % 2, me // 4
     partner = {"tp": me + 1 - 2 * c}
@@ -41,6 +42,7 @@
     nx = {"tp": me + 4 - 8 * xx}
     first, second = (xx, y), (y, xx)
     to_first, to_second = (nx, ny), (ny, nx)
+    to_other = tuple({"tp": d["tp"] + 1 - 2 * c} for d in to_first)
     both = (0, 1)
     i32 = jnp.int32
 
@@ -177,8 +179,34 @@
         arrived(k, AG2)
         go(k, FIN2)
 
+    kl = C - 1
+
+    def lastcp(kind, h, tail, sem, dev):
+        p = ((1 - first[h]) if kind == FIN2 else first[h]) * R2 + (R2 - RT if tail else 0)
+        b = dx.at[pl.ds(al(kl * R + p, RT), RT if tail else R2 - RT), cols(h)]
+        return rc(b, b, kind, sem, dev)
+
+    def count(rows, kind, sem):
+        b = dx.at[pl.ds(0, rows), pl.ds(0, OWN)]
+        return rc(b, b, kind, sem, partner)
+
+    def last2():
+        arrived(kl, AG1)
+        for tail in (False, True):
+            for h in both:
+                lastcp(AG2, h, tail, last.at[0] if tail else recv.at[kl, AG2], to_first[h]).start()
+                if tail:
+                    lastcp(AG2, h, tail, last.at[0], to_other[h]).start()
+        go(kl, FIN1)
+
+    def last3():
+        count(R2 - RT, AG2, recv.at[kl, AG2]).wait_recv()
+        for h in both:
+            lastcp(FIN2, h, False, fin.at[1], partner).start()
+        count(2 * RT, AG2, last.at[0]).wait_recv()
+
     barrier = pltpu.get_barrier_semaphore()
-    for dev in (partner, ny, nx):
+    for dev in (partner, ny, nx, *to_other):
         pl.semaphore_signal(barrier, inc=1, device_id=dev, device_id_type=MESH)
 
     k0 = i32(0)
@@ -198,7 +226,7 @@
     left = jnp.concatenate([acc1[1, 0], acc1[1, 1, :, :HID - HC]], axis=1)
     hidden2(k0, 0, left + dot(dyv[:R, OWN:], dwd[:, OWN:], NT))
     wait(load_w(0))
-    pl.semaphore_wait(barrier, 3)
+    pl.semaphore_wait(barrier, 5)
     term(k0, 0, 0)
     for h in both:
         cp(k0, D2D, h, True).start()
@@ -287,17 +315,26 @@
         for f, k in events[i]:
             f(i32(k))
         piece()
-    for f, k in [(gather2, 6), (gather3, 2), (gather3, 3), (gather3, 4), (gather2, 7), (gather3, 5), (gather3, 6), (gather3, 7)]:
-        f(i32(k))
-
-    for kind, b in sizes.items():
-        w = rc(b, b, kind, fin.at[max(kind - FIN1, 0)], partner)
-        if kind >= FIN1:
-            w.wait_recv()
-        if kind != D2D:
-            w.wait_send()
+    gather2(i32(6))
+    for k in (2, 3, 4):
+        gather3(i32(k))
+    last2()
+    for k in (5, 6):
+        gather3(i32(k))
+    last3()
+
     for slot in range(SS):
         sent(slot)
+    for kind in (RS1, RS2, AG1, FIN1):
+        b = sizes[kind]
+        w = rc(b, b, kind, fin.at[0], partner)
+        w.wait_send()
+        if kind == FIN1:
+            w.wait_recv()
+    count(C * R2 + RT, AG2, fin.at[0]).wait_send()
+    w = count(C * R2 - RT, FIN2, fin.at[1])
+    w.wait_send()
+    w.wait_recv()
 
 
 def put(dx, dw, dwd, o_dx, o_gate, o_up, o_down, sem):
@@ -350,6 +387,7 @@
                 pltpu.SemaphoreType.DMA((7 + SS,)),
                 pltpu.SemaphoreType.DMA((C + 1, 5)),
                 pltpu.SemaphoreType.DMA((2,)),
+                pltpu.SemaphoreType.DMA((1,)),
                 pltpu.SemaphoreType.DMA((9,)),
                 pltpu.SemaphoreType.DMA((2, 3)),
                 pltpu.SemaphoreType.DMA((XS,)),

time: 88 us -> 88 us (level)
  no operation moved by 1% of the time
where the time goes in v6:
time: 88 us; the launch traced here: 87.9 us
  Pallas kernels  87.1 us (99%)
    pallas_call x1, Pallas kernels, step(): pl.pallas_call(kernel, out_shape=[pltpu.VMEM((ROWS, D), BF), pltpu.VMEM((...  80.8 us
    pallas_call x1, Pallas kernels, step(): pl.pallas_call(put, out_shape=[pltpu.HBM(s, BF) for s in shapes], in_spec...  6.27 us

profile of v6, /device:TPU:0, one launch (start us, length us, event | category | flops | bytes accessed | tf_op | source)
XLA Modules:
  0.0 87.9 jit_solution(3778685449300378094)
XLA Ops:
  0.6 80.8 %shard_map.102 = (bf16[2048,2048]{1,0:T(8,128)(2,1)S(1)}, bf16[2048,1536]{1,0:T(8,128)(2,1)S(1)}, bf16[768,2048]{1,0:T(8,128)(2,1)S(1)}) custom-call(bf16[2048,2048]{1,0:T(8,128)(2,1)} %x.1, bf16[2048,2048]{1,0:T(8,128)(2,1)} %dy.1, bf16[2048,768]{1,0:T(8,128)(2,1)} %gate.1, bf16[2048,768]{1,0:T(8,128)(2,1)} %up.1, bf16[2048,768]{1,0:T(8,128)(2,1)} %w_gate.1, ...), custom_call_target="tpu_custom_call" | custom-call | tf_op jit(solution)/shard_map/pallas_call | solution.py:364
  81.5 6.3 %shard_map.103 = (bf16[2048,2048]{1,0:T(8,128)(2,1)}, bf16[2048,768]{1,0:T(8,128)(2,1)}, bf16[2048,768]{1,0:T(8,128)(2,1)}, bf16[768,2048]{1,0:T(8,128)(2,1)}) custom-call(bf16[2048,2048]{1,0:T(8,128)(2,1)S(1)} %get-tuple-element.7.dx, bf16[2048,1536]{1,0:T(8,128)(2,1)S(1)} %get-tuple-element.8.dw, bf16[768,2048]{1,0:T(8,128)(2,1)S(1)} %get-tuple-element.9.dwd), custom_call_target="tpu_custom_call" | custom-call | tf_op jit(solution)/shard_map/pallas_call | solution.py:398
